TPU v7x, 32 devices: a whole 2x2x4 slice. The times are simulated.
32 devices in a mesh: groups: 2 (over x), tile: 16 (over z, y, core).
Axes of the slice: x: 2, y: 2, z: 4, core: 2. Of those that a mesh axis runs over, the one named last changes fastest.
Arguments:
- tracer: float32 [32, 6, 8, 128, 128], P(('groups', 'tile')), parts along dimension 0, may hold values from -6 to 6
- courant_east: bfloat16 [32, 6, 8, 128, 128], P(('groups', 'tile')), parts along dimension 0, may hold values from -1.5 to 1.5
- courant_north: bfloat16 [32, 6, 8, 128, 128], P(('groups', 'tile')), parts along dimension 0, may hold values from -1.5 to 1.5
- diffusivity: bfloat16 [32, 6, 8, 128, 128], P(('groups', 'tile')), parts along dimension 0, may hold values from 0.049804688 to 5
- seam_table: int32 [6, 4, 3], replicated, may hold values from 0 to 5, as said below
Outputs:
- updated: float32 [32, 6, 8, 128, 128], P(('groups', 'tile')), parts along dimension 0
There are 2 independent parts, one for each index of `groups`. A program takes and returns all parts, laid end to end along the dimension named above; an argument that names none is the same for every part. Nothing has to cross between parts.
Inputs may be any that keep to these rules, and one draw needn't show every extreme that they name: seam_table[p, e] = (q, f, r) names the edge f of panel q != p that borders edge e of panel p, and r is 1 where their edge indices run in opposite directions, 0 otherwise; the 24 edges form 12 pairs whose entries name each other with the same r, as on the faces of a cube ; edge 3 of panel 0 borders edge 3 of panel 1.
All inputs are finite; a program needn't handle non-finite values.
Results may differ from a plain program's by a relative error of at most 0.0003.
Values sent between devices are 32-bit elements; how exact they have to be, the bound alone decides.
A program may use at most 128 MiB of HBM per device.

v0:
```python
import math
import jax
import jax.numpy as jnp
from jax import lax
from jax.sharding import PartitionSpec as P

DEPTH = 2


def padded(block, sides, width):
    for axis, dim in sides:
        count = lax.axis_size(axis)
        forward = [(i, i + 1) for i in range(count - 1)]
        forward.append((count - 1, 0))
        backward = [(target, source) for source, target in forward]
        low = lax.ppermute(
            lax.slice_in_dim(block, block.shape[dim] - width, None, axis=dim), axis, forward
        )
        high = lax.ppermute(lax.slice_in_dim(block, 0, width, axis=dim), axis, backward)
        block = jnp.concatenate([low, block, high], axis=dim)
    return block


def from_behind(value, axis, steps):
    count = lax.axis_size(axis)
    pairs = [(source, (source + steps) % count) for source in range(count)]
    return lax.ppermute(value, axis, pairs)


def edge_strips(panels, rows_deep):
    south_rows = jnp.moveaxis(panels[:, :, :, :rows_deep], 3, 1)
    east_rows = jnp.moveaxis(panels[:, :, ::-1, :][:, :, :rows_deep, :], 2, 1)
    north_rows = jnp.moveaxis(panels[:, :, :, ::-1][:, :, :, :rows_deep], 3, 1)
    west_rows = jnp.moveaxis(panels[:, :, :rows_deep, :], 2, 1)
    return jnp.stack([south_rows, east_rows, north_rows, west_rows], axis=1)


def centered(extended, along):
    kept = extended.shape[along] - 4

    def shifted(offset):
        return lax.slice_in_dim(extended, 2 + offset, 2 + offset + kept, axis=along)

    return (8.0 * (shifted(1) - shifted(-1)) - (shifted(2) - shifted(-2))) / 12.0


def advance(panels, ghosts, courant_east, courant_north, diffusivity):
    west_part = jnp.moveaxis(ghosts[:, 3, ::-1], 1, 2)
    east_part = jnp.moveaxis(ghosts[:, 1], 1, 2)
    south_part = jnp.transpose(ghosts[:, 0, ::-1], (0, 2, 3, 1))
    north_part = jnp.transpose(ghosts[:, 2], (0, 2, 3, 1))
    along_first = jnp.concatenate([west_part, panels, east_part], axis=2)
    along_second = jnp.concatenate([south_part, panels, north_part], axis=3)
    forced = panels - (
        courant_east.astype(jnp.float32) * centered(along_first, 2)
        + courant_north.astype(jnp.float32) * centered(along_second, 3)
    )
    coupling = diffusivity.astype(jnp.float32)
    ratios = []
    partial_values = []
    for height in range(panels.shape[1]):
        diagonal = 1.0 + coupling[:, height]
        if height > 0:
            below = coupling[:, height - 1]
            pivot_value = diagonal + below - below * ratios[-1]
            current = (forced[:, height] + below * partial_values[-1]) / pivot_value
        else:
            pivot_value = diagonal
            current = forced[:, height] / pivot_value
        ratios.append(coupling[:, height] / pivot_value)
        partial_values.append(current)
    solved = [partial_values[-1]]
    for height in range(panels.shape[1] - 2, -1, -1):
        solved.insert(0, partial_values[height] + ratios[height] * solved[0])
    return jnp.stack(solved, axis=1)


def panel_tiles(device, across):
    total = across * across
    tile_offset = jnp.arange(6, dtype=jnp.int32) % 2 * (total // 2 + 1)
    return ((device - tile_offset) % total, tile_offset)


def placement(device, across):
    panel_tile, tile_offset = panel_tiles(device, across)
    row_no = panel_tile // across
    col_no = panel_tile % across
    on_edge = jnp.stack(
        [col_no == 0, row_no == across - 1, col_no == across - 1, row_no == 0], axis=1
    ).reshape(24)
    along_edge = jnp.stack([row_no, col_no, row_no, col_no], axis=1).reshape(24)
    return (on_edge, along_edge, panel_tile, tile_offset)


def device_at(edge_no, spot, across):
    return jnp.where(
        edge_no == 0,
        spot * across,
        jnp.where(
            edge_no == 1,
            (across - 1) * across + spot,
            jnp.where(edge_no == 2, spot * across + across - 1, spot),
        ),
    )


def neighbour_step(edge_no, across):
    return jnp.where(
        edge_no == 0, -1, jnp.where(edge_no == 1, across, jnp.where(edge_no == 2, 1, -across))
    )


def sources(seam_table, own_device, across):
    total = across * across
    on_edge, along_edge, panel_tile, tile_offset = placement(own_device, across)
    flat_table = seam_table.reshape(24, 3)
    ghost_edge = jnp.arange(24, dtype=jnp.int32) % 4
    ghost_panel = jnp.arange(24, dtype=jnp.int32) // 4
    turned_spot = jnp.where(flat_table[:, 2] == 1, across - 1 - along_edge, along_edge)
    far_tile = device_at(flat_table[:, 1], turned_spot, across)
    far_device = (far_tile + jnp.take(tile_offset, flat_table[:, 0])) % total
    near_device = (own_device + neighbour_step(ghost_edge, across)) % total
    source_device = jnp.where(on_edge, far_device, near_device)
    source_block = jnp.where(
        on_edge, flat_table[:, 0] * 4 + flat_table[:, 1], ghost_panel * 4 + (ghost_edge + 2) % 4
    )
    reverse_it = jnp.logical_and(on_edge, flat_table[:, 2] == 1)
    return (on_edge, flat_table, source_device, source_block, reverse_it, panel_tile)


def shards(tracer, courant_east, courant_north, diffusivity, seam_table):
    panels = tracer[0]
    tile_count = lax.axis_size("tile")
    across = math.isqrt(tile_count)
    own_device = lax.axis_index("tile")
    strips = edge_strips(panels, DEPTH)
    blocks = strips.reshape((24,) + strips.shape[2:])
    on_edge, flat_table, source_device, source_block, reverse_it, panel_tile = sources(
        seam_table, own_device, across
    )
    row_no = panel_tile // across
    col_no = panel_tile % across
    side_first = jnp.where(col_no == across - 1, 2, 0).astype(jnp.int32)
    side_second = jnp.where(row_no == 0, 3, 1).astype(jnp.int32)
    first_rows = jnp.take_along_axis(strips, side_first[:, None, None, None, None], axis=1)[:, 0]
    second_rows = jnp.take_along_axis(strips, side_second[:, None, None, None, None], axis=1)[:, 0]
    packed = jnp.concatenate([first_rows, second_rows], axis=0)
    collected = lax.all_gather(packed[None], "tile", axis=0, tiled=True)
    slot_in = jnp.where(flat_table[:, 1] % 2 == 0, 0, 6) + flat_table[:, 0]
    picked = jnp.take(
        collected.reshape((tile_count * 12,) + blocks.shape[1:]),
        source_device * 12 + slot_in,
        axis=0,
        mode="clip",
    )
    picked = jnp.where(reverse_it[:, None, None, None], picked[..., ::-1], picked)
    both_rows = jnp.stack([strips[:, 0], strips[:, 2]], axis=0)
    widened = padded(both_rows, (("tile", 0),), 1)
    from_west = from_behind(strips[:, 1], "tile", across)
    from_east = from_behind(strips[:, 3], "tile", -across)
    inside = jnp.stack([widened[0], from_east, widened[3], from_west], axis=1).reshape(blocks.shape)
    ghosts = jnp.where(on_edge[:, None, None, None], picked, inside)
    updated = advance(
        panels, ghosts.reshape(strips.shape), courant_east[0], courant_north[0], diffusivity[0]
    )
    return updated[None]


def solution(mesh):
    placed = (
        P(("groups", "tile"), None, None, None, None),
        P(("groups", "tile"), None, None, None, None),
        P(("groups", "tile"), None, None, None, None),
        P(("groups", "tile"), None, None, None, None),
        P(),
    )
    return jax.shard_map(
        shards,
        mesh=mesh,
        in_specs=placed,
        out_specs=P(("groups", "tile"), None, None, None, None),
        check_vma=False,
    )
```

profile of v0, /device:TPU:0, one launch (start us, length us, event | category | flops | bytes accessed | tf_op | source)
XLA Modules:
  0.0 114.8 jit_solution(10395726204144280213)
XLA Ops:
  6.6 1.1 slice_bitcast_fusion
  7.7 5.5 %fusion.60 = (f32[6,8,128,2]{3,2,1,0:T(8,128)}, f32[6,8,128,2]{3,2,1,0:T(8,128)S(1)}) fusion(f32[6,8,128,128]{3,2,1,0:T(8,128)} %bitcast.97), kind=kLoop, calls=%fused_computation.177 | loop fusion | bytes 196608 | tf_op jit(solution)/shard_map/slice | solution.py:33
  13.2 0.1 slice.139
  13.3 2.4 %copy.55 = f32[6,8,128,2]{2,3,1,0:T(2,128)S(1)} copy(f32[6,8,128,2]{3,2,1,0:T(8,128)} %get-tuple-element.24) | data formatting | bytes 98304
  15.7 0.1 slice.141
  15.8 1.2 %copy.54 = f32[6,8,128,2]{2,3,1,0:T(2,128)S(1)} copy(f32[6,8,128,2]{3,2,1,0:T(8,128)S(1)} %get-tuple-element.25) | data formatting | bytes 98304
  17.1 0.6 gather_fusion.3
  17.7 0.6 gather_fusion.2
  18.6 0.7 copy.44
  19.3 3.1 %collective-permute-start.3 = (f32[6,2,8,128]{3,1,2,0:T(2,128)S(1)}, f32[6,2,8,128]{3,1,2,0:T(2,128)S(1)}, u32[]{:S(2)}, u32[]{:S(2)}) collective-permute-start(f32[6,2,8,128]{3,1,2,0:T(2,128)S(1)} %bitcast.107), channel_id=1, source_target_pairs={{0,4},{1,5},{2,6},{3,7},{4,8},{5,9},{6,10},{7,11},{8,12},{9,13},{1... | collective-permute-start | bytes 147464 | tf_op jit(solution)/shard_map/ppermute | solution.py:27
  22.4 2.1 %collective-permute-start.1 = (f32[6,2,8,128]{3,1,2,0:T(2,128)S(1)}, f32[6,2,8,128]{3,1,2,0:T(2,128)S(1)}, u32[]{:S(2)}, u32[]{:S(2)}) collective-permute-start(f32[6,2,8,128]{3,1,2,0:T(2,128)S(1)} %get-tuple-element.22), channel_id=1, source_target_pairs={{0,12},{1,13},{2,14},{3,15},{4,0},{5,1},{6,2},{7,3},{8,4},{9,5},{1... | collective-permute-start | bytes 147464 | tf_op jit(solution)/shard_map/ppermute | solution.py:27
  24.5 4.4 %collective-permute-start.2 = (f32[1,6,2,8,128]{4,3,2,1,0:T(8,128)S(1)}, f32[1,6,2,8,128]{4,3,2,1,0:T(8,128)S(1)}, u32[]{:S(2)}, u32[]{:S(2)}) collective-permute-start(f32[1,6,2,8,128]{4,3,2,1,0:T(8,128)S(1)} %copy.47), channel_id=1, source_target_pairs={{1,0},{2,1},{3,2},{4,3},{5,4},{6,5},{7,6},{8,7},{9,8},{10,9},{11,1... | collective-permute-start | bytes 147464 | tf_op jit(solution)/shard_map/ppermute | solution.py:19
  29.6 0.7 gather_fusion
  30.4 2.0 %bitcast_convert_fusion = f32[6,8,128,128]{3,2,1,0:T(8,128)} fusion(bf16[1,6,8,128,128]{4,3,2,1,0:T(8,128)(2,1)S(1)} %copy-done.2), kind=kLoop, calls=%fused_computation.34 | loop fusion | flops 786432 | bytes 4718592 | tf_op jit(solution)/shard_map/convert_element_type | solution.py:58
  32.7 29.1 %all-gather.3.cloned.1.call-done = f32[192,2,8,128]{3,2,1,0:T(8,128)} async-done(((f32[12,2,8,128]{3,2,1,0:T(8,128)}), f32[192,2,8,128]{3,2,1,0:T(8,128)}) %all-gather.3.cloned.1.call-update) | async-done | bytes 1572880 | tf_op jit(solution)/shard_map/all_gather | solution.py:148
  61.8 2.0 %gather_fusion.1 = f32[24,2,8,128]{3,2,1,0:T(8,128)S(1)} fusion(f32[192,2,8,128]{3,2,1,0:T(8,128)} %all-gather.3.cloned.1.call-done, s32[1024]{0:T(1024)S(1)} %pad_clamp_fusion), kind=kCustom, calls=%fused_computation.3 | custom fusion | bytes 393312 | tf_op jit(solution)/shard_map/jit(_take)/gather | solution.py:150
  63.8 0.1 bitcast_select_fusion
  64.2 2.2 %copy.58 = f32[6,1,2,8,128]{2,4,3,0,1:T(8,128)} copy(f32[6,1,2,8,128]{4,3,2,1,0:T(8,128)S(1)} %get-tuple-element.26) | data formatting | bytes 98304
  66.4 2.3 %copy.59 = f32[6,1,2,8,128]{2,4,3,0,1:T(8,128)} copy(f32[6,1,2,8,128]{4,3,2,1,0:T(8,128)S(1)} %get-tuple-element.29) | data formatting | bytes 98304
  68.7 26.0 %rev.13 = f32[6,1,2,8,128]{2,4,3,0,1:T(8,128)} reverse(f32[6,1,2,8,128]{2,4,3,0,1:T(8,128)} %copy.59), dimensions={2} | reverse | bytes 98304 | tf_op jit(solution)/shard_map/rev | solution.py:50
  94.6 9.8 %fusion.7 = f32[6,8,128,128]{3,2,1,0:T(8,128)S(1)} fusion(f32[6,8,128,128]{3,2,1,0:T(8,128)S(1)} %bitcast.98, f32[6,8,2,128]{3,2,1,0:T(2,128)S(1)} %bitcast.110, f32[6,8,2,128]{3,2,1,0:T(2,128)S(1)} %bitcast.111, f32[6,8,128,2]{3,2,1,0:T(8,128)} %bitcast.100, f32[6,8,128,2]{3,2,1,0:T(8,128)} %bitcast.99, bf16[1,6,8,128,128]{4,3,2,1,0:T(8,128)(2,1)} %param.9, ...), kind=kLoop, calls=%fused_computation.19 | loop fusion | flops 18874368 | bytes 9633792 | tf_op jit(solution)/shard_map/sub | solution.py:54
  104.5 0.7 fusion.22
  105.2 0.7 add_dynamic-update-slice_fusion
  106.3 1.7 %copy-done.3 = f32[6,8,128,128]{3,2,1,0:T(8,128)} copy-done((f32[6,8,128,128]{3,2,1,0:T(8,128)}, f32[6,8,128,128]{3,2,1,0:T(8,128)S(1)}, u32[]{:S(2)}) %copy-start.3) | copy-done | bytes 3145752
  (60 shorter events, 1.9 us)
Async XLA Ops:
  6.5 55.2 %all-gather.3.cloned.1.call-start = ((), (), s32[]{:S(2)}) async-start(), calls=%async_computation | async-start | bytes 1671168 | tf_op jit(solution)/shard_map/all_gather | solution.py:148
  15.7 13.8 %copy-start.4 = (s32[6,4,3]{0,1,2:T(4,128)S(1)}, s32[6,4,3]{0,1,2:T(4,128)}, u32[]{:S(2)}) copy-start(s32[6,4,3]{0,1,2:T(4,128)} %param.11) | copy-start | bytes 868
  17.0 13.4 %copy-start.2 = (bf16[1,6,8,128,128]{4,3,2,1,0:T(8,128)(2,1)S(1)}, bf16[1,6,8,128,128]{4,3,2,1,0:T(8,128)(2,1)}, u32[]{:S(2)}) copy-start(bf16[1,6,8,128,128]{4,3,2,1,0:T(8,128)(2,1)} %param.10) | copy-start | bytes 4718596
  19.3 13.2 %collective-permute-start.3 = (f32[6,2,8,128]{3,1,2,0:T(2,128)S(1)}, f32[6,2,8,128]{3,1,2,0:T(2,128)S(1)}, u32[]{:S(2)}, u32[]{:S(2)}) collective-permute-start(f32[6,2,8,128]{3,1,2,0:T(2,128)S(1)} %bitcast.107), channel_id=1, source_target_pairs={{0,4},{1,5},{2,6},{3,7},{4,8},{5,9},{6,10},{7,11},{8,12},{9,13},{1... | collective-permute-start | bytes 147464 | tf_op jit(solution)/shard_map/ppermute | solution.py:27
  22.4 10.1 %collective-permute-start.1 = (f32[6,2,8,128]{3,1,2,0:T(2,128)S(1)}, f32[6,2,8,128]{3,1,2,0:T(2,128)S(1)}, u32[]{:S(2)}, u32[]{:S(2)}) collective-permute-start(f32[6,2,8,128]{3,1,2,0:T(2,128)S(1)} %get-tuple-element.22), channel_id=1, source_target_pairs={{0,12},{1,13},{2,14},{3,15},{4,0},{5,1},{6,2},{7,3},{8,4},{9,5},{1... | collective-permute-start | bytes 147464 | tf_op jit(solution)/shard_map/ppermute | solution.py:27
  24.5 8.0 %collective-permute-start = (f32[1,6,2,8,128]{4,3,2,1,0:T(8,128)S(1)}, f32[1,6,2,8,128]{4,3,2,1,0:T(8,128)S(1)}, u32[]{:S(2)}, u32[]{:S(2)}) collective-permute-start(f32[1,6,2,8,128]{4,3,2,1,0:T(8,128)S(1)} %copy.45), channel_id=1, source_target_pairs={{0,1},{1,2},{2,3},{3,4},{4,5},{5,6},{6,7},{7,8},{8,9},{9,10},{10,1... | collective-permute-start | bytes 147464 | tf_op jit(solution)/shard_map/ppermute | solution.py:16
  24.5 8.0 %collective-permute-start.2 = (f32[1,6,2,8,128]{4,3,2,1,0:T(8,128)S(1)}, f32[1,6,2,8,128]{4,3,2,1,0:T(8,128)S(1)}, u32[]{:S(2)}, u32[]{:S(2)}) collective-permute-start(f32[1,6,2,8,128]{4,3,2,1,0:T(8,128)S(1)} %copy.47), channel_id=1, source_target_pairs={{1,0},{2,1},{3,2},{4,3},{5,4},{6,5},{7,6},{8,7},{9,8},{10,9},{11,1... | collective-permute-start | bytes 147464 | tf_op jit(solution)/shard_map/ppermute | solution.py:19
  68.7 26.0 %copy-start = (f32[1,6,8,128,128]{4,3,2,1,0:T(8,128)S(1)}, f32[1,6,8,128,128]{4,3,2,1,0:T(8,128)}, u32[]{:S(2)}) copy-start(f32[1,6,8,128,128]{4,3,2,1,0:T(8,128)} %param.7) | copy-start | bytes 9437188
  94.6 9.9 %copy-start.1 = (f32[6,8,128,128]{3,2,1,0:T(8,128)S(1)}, f32[6,8,128,128]{3,2,1,0:T(8,128)}, u32[]{:S(2)}) copy-start(f32[6,8,128,128]{3,2,1,0:T(8,128)} %bitcast_convert_fusion) | copy-start | bytes 9437188
  106.2 1.7 %copy-start.3 = (f32[6,8,128,128]{3,2,1,0:T(8,128)}, f32[6,8,128,128]{3,2,1,0:T(8,128)S(1)}, u32[]{:S(2)}) copy-start(f32[6,8,128,128]{3,2,1,0:T(8,128)S(1)} %constant_dynamic-update-slice_fusion) | copy-start | bytes 9437188
Sparse Core Ops, SparseCore 0:
  19.4 42.3 all-gather.2
where the time goes:
time: 117 us; the launch traced here: 115 us
  local copies, waits for them, and re-layouts  48 us (41%)
  waiting for transfers between devices  29.1 us (25%)
  other arithmetic  14.3 us (12%)
  between operations  13.7 us (12%)
  starting transfers between devices  9.64 us (8%)
    all_gather x1, waiting for transfers between devices, shards(): collected = lax.all_gather(packed[None], 'tile', axis=0, tiled=True)  29.1 us
    rev x1, local copies, waits for them, and re-layouts, advance(): south_part = jnp.transpose(ghosts[:, 0, ::-1], (0, 2, 3, 1))  26 us
    unnamed x20, local copies, waits for them, and re-layouts  9.93 us
    sub x1, other arithmetic, advance(): panels - (courant_east.astype(jnp.float32) * centered(along_first, 2) + c...  9.84 us
    slice x2, local copies, waits for them, and re-layouts, edge_strips(): north_rows = jnp.moveaxis(panels[:, :, :, ::-1][:, :, :, :rows_deep], 3, 1)  5.6 us
    ppermute x2, starting transfers between devices, from_behind(): return lax.ppermute(value, axis, pairs)  5.2 us
    ppermute x1, starting transfers between devices, padded(): lax.ppermute(lax.slice_in_dim(block, 0, width, axis=dim), axis, backward)  4.44 us
  transfers between devices with their start and end apart: 5, of which 1 were waited for; matrix products, arithmetic and copies ran while one was open for 3% of the time, Pallas kernels for 0%

commit v1 on v0

--- a/solution.py
+++ b/solution.py
@@ -145,7 +145,9 @@
     first_rows = jnp.take_along_axis(strips, side_first[:, None, None, None, None], axis=1)[:, 0]
     second_rows = jnp.take_along_axis(strips, side_second[:, None, None, None, None], axis=1)[:, 0]
     packed = jnp.concatenate([first_rows, second_rows], axis=0)
-    collected = lax.all_gather(packed[None], "tile", axis=0, tiled=True)
+    block_2 = packed[None]
+    stack = jnp.stack([block_2] * lax.axis_size("tile"))
+    collected = jnp.concatenate(lax.all_to_all(stack, "tile", 0, 0), axis=0)
     slot_in = jnp.where(flat_table[:, 1] % 2 == 0, 0, 6) + flat_table[:, 0]
     picked = jnp.take(
         collected.reshape((tile_count * 12,) + blocks.shape[1:]),

time: 117 us -> 105 us (0.90)
  the two profiles are of different devices: /device:TPU:0 before, /device:TPU:12 now
where the time goes in v1:
time: 105 us; the launch traced here: 103 us
  local copies, waits for them, and re-layouts  50 us (48%)
  waiting for transfers between devices  26.7 us (25%)
  other arithmetic  16.4 us (16%)
  starting transfers between devices  10 us (10%)
    ppermute x2, waiting for transfers between devices, from_behind(): return lax.ppermute(value, axis, pairs)  26.7 us
    rev x1, local copies, waits for them, and re-layouts, advance(): south_part = jnp.transpose(ghosts[:, 0, ::-1], (0, 2, 3, 1))  25.9 us
    unnamed x20, local copies, waits for them, and re-layouts  10.6 us
    sub x1, other arithmetic, advance(): panels - (courant_east.astype(jnp.float32) * centered(along_first, 2) + c...  9.74 us
    all_to_all x1, starting transfers between devices, shards(): collected = jnp.concatenate(lax.all_to_all(stack, 'tile', 0, 0), axis=0)  6.24 us
    slice x2, local copies, waits for them, and re-layouts, edge_strips(): north_rows = jnp.moveaxis(panels[:, :, :, ::-1][:, :, :, :rows_deep], 3, 1)  5.6 us
  transfers between devices with their start and end apart: 5, of which 2 were waited for; matrix products, arithmetic and copies ran while one was open for 8% of the time, Pallas kernels for 0%

profile of v1, /device:TPU:12, one launch (start us, length us, event | category | flops | bytes accessed | tf_op | source)
XLA Modules:
  0.0 103.4 jit_solution(2417855888968502306)
XLA Ops:
  0.1 1.1 %slice_bitcast_fusion = (f32[6,1,2,8,128]{4,2,3,0,1:T(2,128)S(1)}, f32[6,2,8,128]{3,1,2,0:T(2,128)S(1)}, f32[6,8,2,128]{3,2,1,0:T(2,128)S(1)}) fusion(f32[6,8,128,128]{3,2,1,0:T(8,128)} %bitcast.97), kind=kLoop, calls=%fused_computation.84 | loop fusion | bytes 245760 | tf_op jit(solution)/shard_map/stack | solution.py:35
  1.1 5.5 %fusion.60 = (f32[6,8,128,2]{3,2,1,0:T(8,128)}, f32[6,8,128,2]{3,2,1,0:T(8,128)S(1)}) fusion(f32[6,8,128,128]{3,2,1,0:T(8,128)} %bitcast.98), kind=kLoop, calls=%fused_computation.177 | loop fusion | bytes 196608 | tf_op jit(solution)/shard_map/slice | solution.py:33
  6.8 2.4 %copy.56 = f32[6,8,128,2]{2,3,1,0:T(2,128)S(1)} copy(f32[6,8,128,2]{3,2,1,0:T(8,128)} %get-tuple-element.24) | data formatting | bytes 98304
  9.3 1.2 %copy.55 = f32[6,8,128,2]{2,3,1,0:T(2,128)S(1)} copy(f32[6,8,128,2]{3,2,1,0:T(8,128)S(1)} %get-tuple-element.25) | data formatting | bytes 98304
  12.1 1.3 %stack.58 = f32[16,1,12,2,8,128]{5,4,3,2,1,0:T(8,128)} broadcast(f32[12,2,8,128]{3,2,1,0:T(8,128)S(1)} %copy.45), dimensions={2,3,4,5} | broadcast | bytes 1671168 | tf_op jit(solution)/shard_map/stack | solution.py:149
  13.4 6.2 %all-to-all-start = ((f32[16,1,12,2,8,128]{5,4,3,2,1,0:T(8,128)}), f32[16,1,12,2,8,128]{5,4,3,2,1,0:T(8,128)S(1)}, u32[]{:S(2)}, u32[]{:S(2)}) async-start(f32[16,1,12,2,8,128]{5,4,3,2,1,0:T(8,128)} %stack.58), calls=%async_computation | async-start | bytes 3145728 | tf_op jit(solution)/shard_map/all_to_all | solution.py:150
  19.6 1.5 %collective-permute-start.3 = (f32[6,2,8,128]{3,1,2,0:T(2,128)S(1)}, f32[6,2,8,128]{3,1,2,0:T(2,128)S(1)}, u32[]{:S(2)}, u32[]{:S(2)}) collective-permute-start(f32[6,2,8,128]{3,1,2,0:T(2,128)S(1)} %bitcast.109), channel_id=1, source_target_pairs={{0,4},{1,5},{2,6},{3,7},{4,8},{5,9},{6,10},{7,11},{8,12},{9,13},{1... | collective-permute-start | bytes 147464 | tf_op jit(solution)/shard_map/ppermute | solution.py:27
  21.7 1.7 %collective-permute-start.2 = (f32[1,6,2,8,128]{4,3,2,1,0:T(8,128)S(1)}, f32[1,6,2,8,128]{4,3,2,1,0:T(8,128)S(1)}, u32[]{:S(2)}, u32[]{:S(2)}) collective-permute-start(f32[1,6,2,8,128]{4,3,2,1,0:T(8,128)S(1)} %copy.48), channel_id=1, source_target_pairs={{1,0},{2,1},{3,2},{4,3},{5,4},{6,5},{7,6},{8,7},{9,8},{10,9},{11,1... | collective-permute-start | bytes 147464 | tf_op jit(solution)/shard_map/ppermute | solution.py:19
  24.2 0.7 reshape.438
  25.6 0.8 copy.42
  26.3 0.7 reshape.437
  27.0 0.7 fusion.54
  27.7 0.7 gather_fusion
  28.4 0.7 bitcast_and_fusion
  29.1 0.8 fusion.51
  29.9 2.0 %bitcast_convert_fusion = f32[6,8,128,128]{3,2,1,0:T(8,128)} fusion(bf16[1,6,8,128,128]{4,3,2,1,0:T(8,128)(2,1)S(1)} %copy-done.2), kind=kLoop, calls=%fused_computation.34 | loop fusion | flops 786432 | bytes 4718592 | tf_op jit(solution)/shard_map/convert_element_type | solution.py:58
  32.1 24.7 %collective-permute-done.3 = f32[6,2,8,128]{3,1,2,0:T(2,128)S(1)} collective-permute-done((f32[6,2,8,128]{3,1,2,0:T(2,128)S(1)}, f32[6,2,8,128]{3,1,2,0:T(2,128)S(1)}, u32[]{:S(2)}, u32[]{:S(2)}) %collective-permute-start.3) | collective-permute-done | bytes 49184 | tf_op jit(solution)/shard_map/ppermute | solution.py:27
  56.8 2.0 %collective-permute-done.1 = f32[6,2,8,128]{3,1,2,0:T(2,128)S(1)} collective-permute-done((f32[6,2,8,128]{3,1,2,0:T(2,128)S(1)}, f32[6,2,8,128]{3,1,2,0:T(2,128)S(1)}, u32[]{:S(2)}, u32[]{:S(2)}) %collective-permute-start.1) | collective-permute-done | bytes 49184 | tf_op jit(solution)/shard_map/ppermute | solution.py:27
  59.9 2.2 %copy.59 = f32[6,1,2,8,128]{2,4,3,0,1:T(8,128)} copy(f32[6,1,2,8,128]{4,3,2,1,0:T(8,128)S(1)} %get-tuple-element.26) | data formatting | bytes 98304
  62.1 2.3 %copy.60 = f32[6,1,2,8,128]{2,4,3,0,1:T(8,128)} copy(f32[6,1,2,8,128]{4,3,2,1,0:T(8,128)S(1)} %get-tuple-element.29) | data formatting | bytes 98304
  64.4 25.9 %rev.13 = f32[6,1,2,8,128]{2,4,3,0,1:T(8,128)} reverse(f32[6,1,2,8,128]{2,4,3,0,1:T(8,128)} %copy.60), dimensions={2} | reverse | bytes 98304 | tf_op jit(solution)/shard_map/rev | solution.py:50
  90.3 9.7 %fusion.7 = f32[6,8,128,128]{3,2,1,0:T(8,128)S(1)} fusion(f32[6,8,128,128]{3,2,1,0:T(8,128)S(1)} %bitcast.99, f32[6,8,2,128]{3,2,1,0:T(2,128)S(1)} %bitcast.112, f32[6,8,2,128]{3,2,1,0:T(2,128)S(1)} %bitcast.113, f32[6,8,128,2]{3,2,1,0:T(8,128)} %bitcast.101, f32[6,8,128,2]{3,2,1,0:T(8,128)} %bitcast.100, bf16[1,6,8,128,128]{4,3,2,1,0:T(8,128)(2,1)} %param.9, ...), kind=kLoop, calls=%fused_computation.19 | loop fusion | flops 18874368 | bytes 9633792 | tf_op jit(solution)/shard_map/sub | solution.py:54
  100.7 0.7 add_dynamic-update-slice_fusion
  101.8 1.7 %copy-done.3 = f32[6,8,128,128]{3,2,1,0:T(8,128)} copy-done((f32[6,8,128,128]{3,2,1,0:T(8,128)}, f32[6,8,128,128]{3,2,1,0:T(8,128)S(1)}, u32[]{:S(2)}) %copy-start.3) | copy-done | bytes 3145752
  (60 shorter events, 6.1 us)
Async XLA Ops:
  11.2 18.7 %copy-start.2 = (bf16[1,6,8,128,128]{4,3,2,1,0:T(8,128)(2,1)S(1)}, bf16[1,6,8,128,128]{4,3,2,1,0:T(8,128)(2,1)}, u32[]{:S(2)}) copy-start(bf16[1,6,8,128,128]{4,3,2,1,0:T(8,128)(2,1)} %param.10) | copy-start | bytes 4718596
  13.4 45.5 %all-to-all-start = ((f32[16,1,12,2,8,128]{5,4,3,2,1,0:T(8,128)}), f32[16,1,12,2,8,128]{5,4,3,2,1,0:T(8,128)S(1)}, u32[]{:S(2)}, u32[]{:S(2)}) async-start(f32[16,1,12,2,8,128]{5,4,3,2,1,0:T(8,128)} %stack.58), calls=%async_computation | async-start | bytes 3145728 | tf_op jit(solution)/shard_map/all_to_all | solution.py:150
  19.6 37.1 %collective-permute-start.3 = (f32[6,2,8,128]{3,1,2,0:T(2,128)S(1)}, f32[6,2,8,128]{3,1,2,0:T(2,128)S(1)}, u32[]{:S(2)}, u32[]{:S(2)}) collective-permute-start(f32[6,2,8,128]{3,1,2,0:T(2,128)S(1)} %bitcast.109), channel_id=1, source_target_pairs={{0,4},{1,5},{2,6},{3,7},{4,8},{5,9},{6,10},{7,11},{8,12},{9,13},{1... | collective-permute-start | bytes 147464 | tf_op jit(solution)/shard_map/ppermute | solution.py:27
  21.1 37.6 %collective-permute-start.1 = (f32[6,2,8,128]{3,1,2,0:T(2,128)S(1)}, f32[6,2,8,128]{3,1,2,0:T(2,128)S(1)}, u32[]{:S(2)}, u32[]{:S(2)}) collective-permute-start(f32[6,2,8,128]{3,1,2,0:T(2,128)S(1)} %get-tuple-element.22), channel_id=1, source_target_pairs={{0,12},{1,13},{2,14},{3,15},{4,0},{5,1},{6,2},{7,3},{8,4},{9,5},{1... | collective-permute-start | bytes 147464 | tf_op jit(solution)/shard_map/ppermute | solution.py:27
  21.7 10.3 %collective-permute-start = (f32[1,6,2,8,128]{4,3,2,1,0:T(8,128)S(1)}, f32[1,6,2,8,128]{4,3,2,1,0:T(8,128)S(1)}, u32[]{:S(2)}, u32[]{:S(2)}) collective-permute-start(f32[1,6,2,8,128]{4,3,2,1,0:T(8,128)S(1)} %copy.46), channel_id=1, source_target_pairs={{0,1},{1,2},{2,3},{3,4},{4,5},{5,6},{6,7},{7,8},{8,9},{9,10},{10,1... | collective-permute-start | bytes 147464 | tf_op jit(solution)/shard_map/ppermute | solution.py:16
  21.7 10.3 %collective-permute-start.2 = (f32[1,6,2,8,128]{4,3,2,1,0:T(8,128)S(1)}, f32[1,6,2,8,128]{4,3,2,1,0:T(8,128)S(1)}, u32[]{:S(2)}, u32[]{:S(2)}) collective-permute-start(f32[1,6,2,8,128]{4,3,2,1,0:T(8,128)S(1)} %copy.48), channel_id=1, source_target_pairs={{1,0},{2,1},{3,2},{4,3},{5,4},{6,5},{7,6},{8,7},{9,8},{10,9},{11,1... | collective-permute-start | bytes 147464 | tf_op jit(solution)/shard_map/ppermute | solution.py:19
  29.9 29.7 %copy-start.4 = (pred[24]{0:T(512)(128)(4,1)S(1)}, pred[24]{0:T(512)(128)(4,1)}, u32[]{:S(2)}) copy-start(pred[24]{0:T(512)(128)(4,1)} %broadcast_in_dim.48) | copy-start | bytes 76
  64.4 25.9 %copy-start = (f32[1,6,8,128,128]{4,3,2,1,0:T(8,128)S(1)}, f32[1,6,8,128,128]{4,3,2,1,0:T(8,128)}, u32[]{:S(2)}) copy-start(f32[1,6,8,128,128]{4,3,2,1,0:T(8,128)} %param.7) | copy-start | bytes 9437188
  90.3 9.8 %copy-start.1 = (f32[6,8,128,128]{3,2,1,0:T(8,128)S(1)}, f32[6,8,128,128]{3,2,1,0:T(8,128)}, u32[]{:S(2)}) copy-start(f32[6,8,128,128]{3,2,1,0:T(8,128)} %bitcast_convert_fusion) | copy-start | bytes 9437188
  101.8 1.7 %copy-start.3 = (f32[6,8,128,128]{3,2,1,0:T(8,128)}, f32[6,8,128,128]{3,2,1,0:T(8,128)S(1)}, u32[]{:S(2)}) copy-start(f32[6,8,128,128]{3,2,1,0:T(8,128)S(1)} %constant_dynamic-update-slice_fusion) | copy-start | bytes 9437188
